TPU v7x, 512 devices: a whole 4x8x8 slice. The times are simulated.
512 devices in a mesh: heads: 8 (over y_lo, x), blk: 64 (over y_hi, z, core).
Axes of the slice: x: 4, y: 8 (y_hi: 4, y_lo: 2; y = y_hi * 2 + y_lo), z: 8, core: 2. Of those that a mesh axis runs over, the one named last changes fastest.
Arguments:
- queries: bfloat16 [4096, 64, 128], P('blk', 'heads'), may hold values from -8 to 8
- prefix_keys: bfloat16 [8, 131072, 128], P('heads', 'blk'), may hold values from -8 to 8
- cached_prefix_values: bfloat16 [8, 131072, 128], P('heads', 'blk'), may hold values from -6 to 6
- shard_len: int32 [64], replicated, may hold values from 512 to 2048
- reach: int32 [64], replicated, may hold values from 4096 to 8192
- w_out: bfloat16 [8192, 16384], P('heads', 'blk'), may hold values from -0.0625 to 0.0625
Outputs:
- projected: bfloat16 [4096, 16384], P('heads', 'blk')
All inputs are finite; a program needn't handle non-finite values.
Results may differ from a plain program's by a relative error of at most 0.0056.
Values may be sent and summed in bfloat16 or wider, within the bound.
No kernel may reach another device: no remote copies, remote signals or barrier semaphores. Data moves between devices by JAX's collectives and lax.ppermute only.
A program may use at most 64 MiB of HBM per device.

v0:
```python
import jax
import jax.numpy as jnp
from jax import lax
from jax.sharding import Mesh
from jax.sharding import PartitionSpec as P

SPAN = 4
HEADS = ("heads_0", "heads_1")
masked_score = -1e30


def passed_along(value, axis, steps):
    count = lax.axis_size(axis)
    pairs = [(source, (source + steps) % count) for source in range(count)]
    return lax.ppermute(value, axis, pairs)


def split_up(value, dim, length):
    lengths = value.shape
    blocks = value.reshape(*lengths[:dim], length, lengths[dim] // length, *lengths[dim + 1 :])
    return jnp.moveaxis(blocks, dim, 0)


def joined_along(blocks, dim):
    lengths = list(blocks.shape[1:])
    lengths[dim] *= blocks.shape[0]
    return jnp.moveaxis(blocks, 0, dim).reshape(lengths)


def exchange_in_order(blocks, axes, turns):
    lengths = [lax.axis_size(a) for a in axes]
    blocks = blocks.reshape(*lengths, *blocks.shape[1:])
    for k in turns:
        blocks = lax.all_to_all(blocks, axes[k], split_axis=k, concat_axis=k, tiled=True)
    return blocks.reshape(-1, *blocks.shape[len(axes) :])


def stepwise_exchange(value, axes, turns, split_dim, concat_dim):
    blocks = split_up(value, split_dim, lax.axis_size(axes))
    return joined_along(exchange_in_order(blocks, axes, turns), concat_dim)


def part_stats(query_tile_rows, key_block, value_block, visible):
    head_size = query_tile_rows.shape[-1]
    scores = jnp.einsum(
        "thgd,hnd->thgn", query_tile_rows, key_block, preferred_element_type=jnp.float32
    ) * head_size ** (-0.5)
    visible_grid = visible[:, None, None, :]
    maxima = jnp.max(jnp.where(visible_grid, scores, masked_score), axis=-1)
    weights = jnp.where(visible_grid, jnp.exp(scores - maxima[..., None]), 0.0)
    totals = jnp.sum(weights, axis=-1)
    weighted = jnp.einsum(
        "thgn,hnd->thgd",
        weights.astype(jnp.bfloat16),
        value_block,
        preferred_element_type=jnp.float32,
    )
    return (maxima, totals, weighted)


def combine_parts(first, second):
    joined = jnp.maximum(first[0], second[0])
    first_factor = jnp.exp(first[0] - joined)
    second_factor = jnp.exp(second[0] - joined)
    totals = first[1] * first_factor + second[1] * second_factor
    weighted = first[2] * first_factor[..., None] + second[2] * second_factor[..., None]
    return (joined, totals, weighted)


def on_device(queries, prefix_keys, cached_prefix_values, shard_len, reach, w_out):
    shard_count = lax.axis_size("blk")
    group_count = lax.axis_size(HEADS)
    own_index = lax.axis_index("blk")
    query_len = queries.shape[0]
    heads_local = queries.shape[1]
    head_size = queries.shape[2]
    kv_local = prefix_keys.shape[0]
    keys_len = prefix_keys.shape[1]
    columns = w_out.shape[1]
    full_weight = lax.all_gather(w_out, HEADS, axis=0, tiled=True)
    local_queries = queries.reshape(query_len, kv_local, heads_local // kv_local, head_size)
    row_ids = jnp.arange(query_len, dtype=jnp.int32)[:, None]
    slot_ids = jnp.arange(keys_len, dtype=jnp.int32)[None, :]

    def mask_for(block_id, shard_id, offset):
        return (slot_ids < shard_len[shard_id]) & (
            offset * keys_len + slot_ids < reach[block_id] + row_ids
        )

    running = part_stats(
        local_queries, prefix_keys, cached_prefix_values, mask_for(own_index, own_index, 0)
    )
    for offset in range(1, SPAN):
        visitor = passed_along(local_queries, "blk", offset)
        owner_id = (own_index - offset + shard_count) % shard_count
        maxima, totals, weighted = part_stats(
            visitor, prefix_keys, cached_prefix_values, mask_for(owner_id, own_index, offset)
        )
        returned = passed_along((maxima, totals, weighted), "blk", -offset)
        running = combine_parts(running, returned)
    attended = (
        (running[2] / running[1][..., None])
        .astype(jnp.bfloat16)
        .reshape(query_len, heads_local * head_size)
    )
    share_rows = stepwise_exchange(attended, HEADS, (0, 1), 0, 1)
    strided = jnp.dot(
        lax.all_gather(share_rows, "blk", axis=0, tiled=True),
        full_weight,
        preferred_element_type=jnp.float32,
    ).astype(jnp.bfloat16)
    share_len = share_rows.shape[0]
    grouped = strided.reshape(group_count, shard_count // group_count, 1, share_len, columns)
    ordered = lax.all_to_all(grouped, HEADS, split_axis=0, concat_axis=2, tiled=True)
    return ordered.reshape(shard_count // group_count * group_count * share_len, columns)


def solution(mesh):
    finer = Mesh(mesh.devices.reshape(2, 4, mesh.shape["blk"]), ("heads_0", "heads_1", "blk"))
    placed = (
        P("blk", HEADS, None),
        P(HEADS, "blk", None),
        P(HEADS, "blk", None),
        P(),
        P(),
        P(HEADS, "blk"),
    )
    return jax.shard_map(
        on_device, mesh=finer, in_specs=placed, out_specs=P(HEADS, "blk"), check_vma=False
    )
```

profile of v0, /device:TPU:16, one launch (start us, length us, event | category | flops | bytes accessed | tf_op | source)
XLA Modules:
  0.0 239.9 jit_solution(17325042349350337519)
XLA Ops:
  8.2 3.7 %collective-permute-start.6 = (bf16[64,1,8,128]{3,0,2,1:T(8,128)(2,1)S(1)}, bf16[64,1,8,128]{3,0,2,1:T(8,128)(2,1)S(1)}, u32[]{:S(2)}, u32[]{:S(2)}) collective-permute-start(bf16[64,1,8,128]{3,0,2,1:T(8,128)(2,1)S(1)} %bitcast.279), channel_id=1, source_target_pairs={{0,3},{1,4},{2,5},{3,6},{4,7},{5,8},{6,9},{7,10},{8,11},{9,12},{10... | collective-permute-start | bytes 393224 | tf_op jit(solution)/shard_map/ppermute | solution.py:15
  12.0 4.3 %collective-permute-start.3 = (bf16[64,1,8,128]{3,0,2,1:T(8,128)(2,1)S(1)}, bf16[64,1,8,128]{3,0,2,1:T(8,128)(2,1)S(1)}, u32[]{:S(2)}, u32[]{:S(2)}) collective-permute-start(bf16[64,1,8,128]{3,0,2,1:T(8,128)(2,1)S(1)} %bitcast.280), channel_id=1, source_target_pairs={{0,2},{1,3},{2,4},{3,5},{4,6},{5,7},{6,8},{7,9},{8,10},{9,11},{10,... | collective-permute-start | bytes 393224 | tf_op jit(solution)/shard_map/ppermute | solution.py:15
  16.2 4.1 %collective-permute-start = (bf16[64,1,8,128]{3,0,2,1:T(8,128)(2,1)S(1)}, bf16[64,1,8,128]{3,0,2,1:T(8,128)(2,1)S(1)}, u32[]{:S(2)}, u32[]{:S(2)}) collective-permute-start(bf16[64,1,8,128]{3,0,2,1:T(8,128)(2,1)S(1)} %bitcast.281), channel_id=1, source_target_pairs={{0,1},{1,2},{2,3},{3,4},{4,5},{5,6},{6,7},{7,8},{8,9},{9,10},{10,1... | collective-permute-start | bytes 393224 | tf_op jit(solution)/shard_map/ppermute | solution.py:15
  20.4 1.3 dynamic_slice.18
  21.7 1.5 fusion.99
  24.4 1.3 iota_add_fusion.3
  26.9 1.8 fusion.9
  28.7 2.2 collective-permute-done
  33.0 2.2 collective-permute-start.9
  35.2 2.1 collective-permute-start.1
  39.4 3.9 %collective-permute-start.10 = (f32[64,1,8]{0,2,1:T(8,128)S(1)}, f32[64,1,8]{0,2,1:T(8,128)S(1)}, u32[]{:S(2)}, u32[]{:S(2)}) collective-permute-start(f32[64,1,8]{0,2,1:T(8,128)S(1)} %bitcast.286), channel_id=1, source_target_pairs={{0,62},{1,63},{2,0},{3,1},{4,2},{5,3},{6,4},{7,5},{8,6},{9,7},{10,... | collective-permute-start | bytes 6152 | tf_op jit(solution)/shard_map/ppermute | solution.py:15
  43.3 3.5 %collective-permute-start.4 = (f32[64,1,8]{0,2,1:T(8,128)S(1)}, f32[64,1,8]{0,2,1:T(8,128)S(1)}, u32[]{:S(2)}, u32[]{:S(2)}) collective-permute-start(f32[64,1,8]{0,2,1:T(8,128)S(1)} %bitcast.283), channel_id=1, source_target_pairs={{0,62},{1,63},{2,0},{3,1},{4,2},{5,3},{6,4},{7,5},{8,6},{9,7},{10,... | collective-permute-start | bytes 6152 | tf_op jit(solution)/shard_map/ppermute | solution.py:15
  51.6 2.9 %collective-permute-start.2 = (f32[64,1,8,128]{3,0,2,1:T(8,128)S(1)}, f32[64,1,8,128]{3,0,2,1:T(8,128)S(1)}, u32[]{:S(2)}, u32[]{:S(2)}) collective-permute-start(f32[64,1,8,128]{3,0,2,1:T(8,128)S(1)} %fusion.42), channel_id=1, source_target_pairs={{0,63},{1,0},{2,1},{3,2},{4,3},{5,4},{6,5},{7,6},{8,7},{9,8},{10,9... | collective-permute-start | bytes 786440 | tf_op jit(solution)/shard_map/ppermute | solution.py:15
  54.5 3.7 %collective-permute-start.5 = (f32[64,1,8,128]{3,0,2,1:T(8,128)S(1)}, f32[64,1,8,128]{3,0,2,1:T(8,128)S(1)}, u32[]{:S(2)}, u32[]{:S(2)}) collective-permute-start(f32[64,1,8,128]{3,0,2,1:T(8,128)S(1)} %fusion.39), channel_id=1, source_target_pairs={{0,62},{1,63},{2,0},{3,1},{4,2},{5,3},{6,4},{7,5},{8,6},{9,7},{10,... | collective-permute-start | bytes 786440 | tf_op jit(solution)/shard_map/ppermute | solution.py:15
  58.2 2.4 %collective-permute-start.11 = (f32[64,1,8]{0,2,1:T(8,128)S(1)}, f32[64,1,8]{0,2,1:T(8,128)S(1)}, u32[]{:S(2)}, u32[]{:S(2)}) collective-permute-start(f32[64,1,8]{0,2,1:T(8,128)S(1)} %bitcast.287), channel_id=1, source_target_pairs={{0,61},{1,62},{2,63},{3,0},{4,1},{5,2},{6,3},{7,4},{8,5},{9,6},{10... | collective-permute-start | bytes 6152 | tf_op jit(solution)/shard_map/ppermute | solution.py:15
  60.6 2.4 collective-permute-start.7
  63.0 7.1 %collective-permute-start.8 = (f32[64,1,8,128]{3,0,2,1:T(8,128)S(1)}, f32[64,1,8,128]{3,0,2,1:T(8,128)S(1)}, u32[]{:S(2)}, u32[]{:S(2)}) collective-permute-start(f32[64,1,8,128]{3,0,2,1:T(8,128)S(1)} %fusion.36), channel_id=1, source_target_pairs={{0,61},{1,62},{2,63},{3,0},{4,1},{5,2},{6,3},{7,4},{8,5},{9,6},{10... | collective-permute-start | bytes 786440 | tf_op jit(solution)/shard_map/ppermute | solution.py:15
  71.3 8.1 %collective-permute-done.8 = f32[64,1,8,128]{3,0,2,1:T(8,128)S(1)} collective-permute-done((f32[64,1,8,128]{3,0,2,1:T(8,128)S(1)}, f32[64,1,8,128]{3,0,2,1:T(8,128)S(1)}, u32[]{:S(2)}, u32[]{:S(2)}) %collective-permute-start.8) | collective-permute-done | bytes 262176 | tf_op jit(solution)/shard_map/ppermute | solution.py:15
  79.3 1.4 fusion.66
  80.9 23.8 %all_to_all.25 = bf16[2,4,8,1024]{3,2,1,0:T(8,128)(2,1)S(1)} all-to-all(bf16[2,4,8,1024]{3,2,1,0:T(8,128)(2,1)S(1)} %reshape_reshape_reshape.3), channel_id=1, replica_groups=mesh['heads_0'=2,'heads_1'=4,'blk'=64] {'heads_0'}, dimensions={0} | all-to-all | bytes 262144 | tf_op jit(solution)/shard_map/all_to_all | solution.py:34
  104.7 9.7 %all_to_all.26 = bf16[2,4,8,1024]{3,2,0,1:T(8,128)(2,1)S(1)} all-to-all(bf16[2,4,8,1024]{3,2,0,1:T(8,128)(2,1)S(1)} %copy.44), channel_id=1, replica_groups=mesh['heads_0'=2,'heads_1'=4,'blk'=64] {'heads_1'}, dimensions={1} | all-to-all | bytes 262144 | tf_op jit(solution)/shard_map/all_to_all | solution.py:34
  115.1 95.9 %all-gather.3.cloned.1.call-done = bf16[512,8192]{1,0:T(8,128)(2,1)} async-done(((bf16[8,8192]{1,0:T(8,128)(2,1)}), bf16[512,8192]{1,0:T(8,128)(2,1)}) %all-gather.3.cloned.1.call-update) | async-done | bytes 8388624 | tf_op jit(solution)/shard_map/all_gather | solution.py:108
  211.0 6.9 %convolution_convert_fusion = bf16[512,256]{1,0:T(8,128)(2,1)S(1)} fusion(bf16[512,8192]{1,0:T(8,128)(2,1)} %all-gather.3.cloned.1.call-done, bf16[8192,256]{1,0:T(8,128)(2,1)} %all-gather.5.cloned.1.call-done), kind=kOutput, calls=%fused_computation.40 | convolution fusion | flops 2147614720 | bytes 12845056 | tf_op jit(solution)/shard_map/dot_general | solution.py:107
  217.9 14.4 %all_to_all.27 = bf16[8,8,1,8,256]{4,3,1,2,0:T(8,128)(2,1)S(1)} all-to-all(bf16[8,8,1,8,256]{4,3,1,2,0:T(8,128)(2,1)S(1)} %bitcast.278), channel_id=1, replica_groups=mesh['heads_0'=2,'heads_1'=4,'blk'=64] {'heads_0','heads_1'}, dimensions={0} | all-to-all | bytes 524288 | tf_op jit(solution)/shard_map/all_to_all | solution.py:114
  (41 shorter events, 15.5 us)
Async XLA Ops:
  6.5 20.4 %copy-start = (bf16[1,2048,128]{2,1,0:T(8,128)(2,1)S(1)}, bf16[1,2048,128]{2,1,0:T(8,128)(2,1)}, u32[]{:S(2)}) copy-start(bf16[1,2048,128]{2,1,0:T(8,128)(2,1)} %param.7) | copy-start | bytes 1572868
  6.5 108.6 %all-gather.5.cloned.1.call-start = ((), (), s32[]{:S(2)}) async-start(), calls=%async_computation.4 | async-start | bytes 4718592 | tf_op jit(solution)/shard_map/all_gather | solution.py:80
  7.3 203.8 %all-gather.3.cloned.1.call-start = ((), (), s32[]{:S(2)}) async-start(), calls=%async_computation.3 | async-start | bytes 8519680 | tf_op jit(solution)/shard_map/all_gather | solution.py:108
  8.2 38.6 %collective-permute-start.6 = (bf16[64,1,8,128]{3,0,2,1:T(8,128)(2,1)S(1)}, bf16[64,1,8,128]{3,0,2,1:T(8,128)(2,1)S(1)}, u32[]{:S(2)}, u32[]{:S(2)}) collective-permute-start(bf16[64,1,8,128]{3,0,2,1:T(8,128)(2,1)S(1)} %bitcast.279), channel_id=1, source_target_pairs={{0,3},{1,4},{2,5},{3,6},{4,7},{5,8},{6,9},{7,10},{8,11},{9,12},{10... | collective-permute-start | bytes 393224 | tf_op jit(solution)/shard_map/ppermute | solution.py:15
  12.0 25.4 %collective-permute-start.3 = (bf16[64,1,8,128]{3,0,2,1:T(8,128)(2,1)S(1)}, bf16[64,1,8,128]{3,0,2,1:T(8,128)(2,1)S(1)}, u32[]{:S(2)}, u32[]{:S(2)}) collective-permute-start(bf16[64,1,8,128]{3,0,2,1:T(8,128)(2,1)S(1)} %bitcast.280), channel_id=1, source_target_pairs={{0,2},{1,3},{2,4},{3,5},{4,6},{5,7},{6,8},{7,9},{8,10},{9,11},{10,... | collective-permute-start | bytes 393224 | tf_op jit(solution)/shard_map/ppermute | solution.py:15
  16.2 14.7 %collective-permute-start = (bf16[64,1,8,128]{3,0,2,1:T(8,128)(2,1)S(1)}, bf16[64,1,8,128]{3,0,2,1:T(8,128)(2,1)S(1)}, u32[]{:S(2)}, u32[]{:S(2)}) collective-permute-start(bf16[64,1,8,128]{3,0,2,1:T(8,128)(2,1)S(1)} %bitcast.281), channel_id=1, source_target_pairs={{0,1},{1,2},{2,3},{3,4},{4,5},{5,6},{6,7},{7,8},{8,9},{9,10},{10,1... | collective-permute-start | bytes 393224 | tf_op jit(solution)/shard_map/ppermute | solution.py:15
  33.0 21.5 %collective-permute-start.9 = (f32[64,1,8]{0,2,1:T(8,128)S(1)}, f32[64,1,8]{0,2,1:T(8,128)S(1)}, u32[]{:S(2)}, u32[]{:S(2)}) collective-permute-start(f32[64,1,8]{0,2,1:T(8,128)S(1)} %bitcast.285), channel_id=1, source_target_pairs={{0,63},{1,0},{2,1},{3,2},{4,3},{5,4},{6,5},{7,6},{8,7},{9,8},{10,9... | collective-permute-start | bytes 6152 | tf_op jit(solution)/shard_map/ppermute | solution.py:15
  35.2 22.9 %collective-permute-start.1 = (f32[64,1,8]{0,2,1:T(8,128)S(1)}, f32[64,1,8]{0,2,1:T(8,128)S(1)}, u32[]{:S(2)}, u32[]{:S(2)}) collective-permute-start(f32[64,1,8]{0,2,1:T(8,128)S(1)} %bitcast.282), channel_id=1, source_target_pairs={{0,63},{1,0},{2,1},{3,2},{4,3},{5,4},{6,5},{7,6},{8,7},{9,8},{10,9... | collective-permute-start | bytes 6152 | tf_op jit(solution)/shard_map/ppermute | solution.py:15
  39.4 8.3 %copy-start.1 = (bf16[1,2048,128]{2,1,0:T(8,128)(2,1)S(1)}, bf16[1,2048,128]{2,1,0:T(8,128)(2,1)}, u32[]{:S(2)}) copy-start(bf16[1,2048,128]{2,1,0:T(8,128)(2,1)} %param.8) | copy-start | bytes 1572868
  39.4 21.2 %collective-permute-start.10 = (f32[64,1,8]{0,2,1:T(8,128)S(1)}, f32[64,1,8]{0,2,1:T(8,128)S(1)}, u32[]{:S(2)}, u32[]{:S(2)}) collective-permute-start(f32[64,1,8]{0,2,1:T(8,128)S(1)} %bitcast.286), channel_id=1, source_target_pairs={{0,62},{1,63},{2,0},{3,1},{4,2},{5,3},{6,4},{7,5},{8,6},{9,7},{10,... | collective-permute-start | bytes 6152 | tf_op jit(solution)/shard_map/ppermute | solution.py:15
  43.3 19.7 %collective-permute-start.4 = (f32[64,1,8]{0,2,1:T(8,128)S(1)}, f32[64,1,8]{0,2,1:T(8,128)S(1)}, u32[]{:S(2)}, u32[]{:S(2)}) collective-permute-start(f32[64,1,8]{0,2,1:T(8,128)S(1)} %bitcast.283), channel_id=1, source_target_pairs={{0,62},{1,63},{2,0},{3,1},{4,2},{5,3},{6,4},{7,5},{8,6},{9,7},{10,... | collective-permute-start | bytes 6152 | tf_op jit(solution)/shard_map/ppermute | solution.py:15
  51.6 19.7 %collective-permute-start.2 = (f32[64,1,8,128]{3,0,2,1:T(8,128)S(1)}, f32[64,1,8,128]{3,0,2,1:T(8,128)S(1)}, u32[]{:S(2)}, u32[]{:S(2)}) collective-permute-start(f32[64,1,8,128]{3,0,2,1:T(8,128)S(1)} %fusion.42), channel_id=1, source_target_pairs={{0,63},{1,0},{2,1},{3,2},{4,3},{5,4},{6,5},{7,6},{8,7},{9,8},{10,9... | collective-permute-start | bytes 786440 | tf_op jit(solution)/shard_map/ppermute | solution.py:15
  54.5 16.8 %collective-permute-start.5 = (f32[64,1,8,128]{3,0,2,1:T(8,128)S(1)}, f32[64,1,8,128]{3,0,2,1:T(8,128)S(1)}, u32[]{:S(2)}, u32[]{:S(2)}) collective-permute-start(f32[64,1,8,128]{3,0,2,1:T(8,128)S(1)} %fusion.39), channel_id=1, source_target_pairs={{0,62},{1,63},{2,0},{3,1},{4,2},{5,3},{6,4},{7,5},{8,6},{9,7},{10,... | collective-permute-start | bytes 786440 | tf_op jit(solution)/shard_map/ppermute | solution.py:15
  58.2 13.0 %collective-permute-start.11 = (f32[64,1,8]{0,2,1:T(8,128)S(1)}, f32[64,1,8]{0,2,1:T(8,128)S(1)}, u32[]{:S(2)}, u32[]{:S(2)}) collective-permute-start(f32[64,1,8]{0,2,1:T(8,128)S(1)} %bitcast.287), channel_id=1, source_target_pairs={{0,61},{1,62},{2,63},{3,0},{4,1},{5,2},{6,3},{7,4},{8,5},{9,6},{10... | collective-permute-start | bytes 6152 | tf_op jit(solution)/shard_map/ppermute | solution.py:15
  60.6 10.6 %collective-permute-start.7 = (f32[64,1,8]{0,2,1:T(8,128)S(1)}, f32[64,1,8]{0,2,1:T(8,128)S(1)}, u32[]{:S(2)}, u32[]{:S(2)}) collective-permute-start(f32[64,1,8]{0,2,1:T(8,128)S(1)} %bitcast.284), channel_id=1, source_target_pairs={{0,61},{1,62},{2,63},{3,0},{4,1},{5,2},{6,3},{7,4},{8,5},{9,6},{10... | collective-permute-start | bytes 6152 | tf_op jit(solution)/shard_map/ppermute | solution.py:15
  63.0 16.4 %collective-permute-start.8 = (f32[64,1,8,128]{3,0,2,1:T(8,128)S(1)}, f32[64,1,8,128]{3,0,2,1:T(8,128)S(1)}, u32[]{:S(2)}, u32[]{:S(2)}) collective-permute-start(f32[64,1,8,128]{3,0,2,1:T(8,128)S(1)} %fusion.36), channel_id=1, source_target_pairs={{0,61},{1,62},{2,63},{3,0},{4,1},{5,2},{6,3},{7,4},{8,5},{9,6},{10... | collective-permute-start | bytes 786440 | tf_op jit(solution)/shard_map/ppermute | solution.py:15
Sparse Core Ops, SparseCore 0:
  9.4 88.5 all-gather.4
  115.2 95.7 all-gather.2
where the time goes:
time: 241 us; the launch traced here: 240 us
  waiting for transfers between devices  107 us (44%)
  blocking collectives  47.9 us (20%)
  starting transfers between devices  42.3 us (18%)
  matrix products  15.5 us (6%)
  between operations  13.7 us (6%)
  other arithmetic  8.18 us (3%)
  local copies, waits for them, and re-layouts  5.26 us (2%)
    all_gather x1, waiting for transfers between devices, on_device(): lax.all_gather(share_rows, 'blk', axis=0, tiled=True)  95.9 us
    ppermute x12, starting transfers between devices, passed_along(): return lax.ppermute(value, axis, pairs)  42.3 us
    all_to_all x2, blocking collectives, exchange_in_order(): lax.all_to_all(blocks, axes[k], split_axis=k, concat_axis=k, tiled=True)  33.5 us
    all_to_all x1, blocking collectives, on_device(): lax.all_to_all(grouped, HEADS, split_axis=0, concat_axis=2, tiled=True)  14.4 us
    ppermute x12, waiting for transfers between devices, passed_along(): return lax.ppermute(value, axis, pairs)  10.3 us
    dot_general x1, matrix products, on_device(): jnp.dot(lax.all_gather(share_rows, 'blk', axis=0, tiled=True), full_weigh...  6.9 us
  transfers between devices with their start and end apart: 14, of which 3 were waited for; matrix products, arithmetic and copies ran while one was open for 9% of the time, Pallas kernels for 0%

commit v1 on v0

--- a/solution.py
+++ b/solution.py
@@ -105,7 +105,9 @@
     )
     share_rows = stepwise_exchange(attended, HEADS, (0, 1), 0, 1)
     strided = jnp.dot(
-        lax.all_gather(share_rows, "blk", axis=0, tiled=True),
+        jnp.concatenate(
+            lax.all_to_all(jnp.stack([share_rows] * lax.axis_size("blk")), "blk", 0, 0), axis=0
+        ),
         full_weight,
         preferred_element_type=jnp.float32,
     ).astype(jnp.bfloat16)

time: 241 us -> 409 us (1.70)
  the two profiles are of different devices: /device:TPU:16 before, /device:TPU:272 now
where the time goes in v1:
time: 409 us; the launch traced here: 408 us
  waiting for transfers between devices  255 us (62%)
  starting transfers between devices  60.7 us (15%)
  blocking collectives  46.2 us (11%)
  matrix products  15.4 us (4%)
  between operations  13.7 us (3%)
  local copies, waits for them, and re-layouts  8.96 us (2%)
  other arithmetic  8.02 us (2%)
    all_gather x1, waiting for transfers between devices, on_device(): full_weight = lax.all_gather(w_out, HEADS, axis=0, tiled=True)  177 us
    all_to_all x1, waiting for transfers between devices, on_device(): lax.all_to_all(jnp.stack([share_rows] * lax.axis_size('blk')), 'blk', 0, 0)  68 us
    ppermute x12, starting transfers between devices, passed_along(): return lax.ppermute(value, axis, pairs)  36.1 us
    all_to_all x1, blocking collectives, on_device(): lax.all_to_all(grouped, HEADS, split_axis=0, concat_axis=2, tiled=True)  29 us
    all_to_all x1, starting transfers between devices, on_device(): lax.all_to_all(jnp.stack([share_rows] * lax.axis_size('blk')), 'blk', 0, 0)  24.5 us
    all_to_all x2, blocking collectives, exchange_in_order(): lax.all_to_all(blocks, axes[k], split_axis=k, concat_axis=k, tiled=True)  17.2 us
    ppermute x12, waiting for transfers between devices, passed_along(): return lax.ppermute(value, axis, pairs)  9.85 us
  transfers between devices with their start and end apart: 14, of which 4 were waited for; matrix products, arithmetic and copies ran while one was open for 4% of the time, Pallas kernels for 0%

profile of v1, /device:TPU:272, one launch (start us, length us, event | category | flops | bytes accessed | tf_op | source)
XLA Modules:
  0.0 408.0 jit_solution(4212525304359693174)
XLA Ops:
  7.5 3.4 collective-permute-start.3
  10.9 2.5 collective-permute-start.6
  13.5 3.8 collective-permute-start
  19.2 1.5 fusion.104
  23.6 1.8 fusion.11
  31.4 3.7 collective-permute-start.10
  37.1 1.9 collective-permute-start.11
  39.0 2.7 collective-permute-start.9
  41.8 1.9 collective-permute-start.1
  44.6 2.3 collective-permute-start.4
  46.9 3.4 collective-permute-start.7
  50.3 3.6 collective-permute-start.2
  54.0 3.4 collective-permute-start.5
  57.4 3.5 collective-permute-start.8
  62.0 3.1 collective-permute-done.5
  65.1 6.8 %collective-permute-done.8 = f32[64,1,8,128]{3,0,2,1:T(8,128)S(1)} collective-permute-done((f32[64,1,8,128]{3,0,2,1:T(8,128)S(1)}, f32[64,1,8,128]{3,0,2,1:T(8,128)S(1)}, u32[]{:S(2)}, u32[]{:S(2)}) %collective-permute-start.8) | collective-permute-done | bytes 262176 | tf_op jit(solution)/shard_map/ppermute | solution.py:15
  73.4 7.1 %all_to_all.30 = bf16[2,4,8,1024]{3,2,1,0:T(8,128)(2,1)S(1)} all-to-all(bf16[2,4,8,1024]{3,2,1,0:T(8,128)(2,1)S(1)} %reshape_reshape_reshape.3), channel_id=1, replica_groups=mesh['heads_0'=2,'heads_1'=4,'blk'=64] {'heads_0'}, dimensions={0} | all-to-all | bytes 262144 | tf_op jit(solution)/shard_map/all_to_all | solution.py:34
  80.5 10.1 %all_to_all.31 = bf16[2,4,8,1024]{3,2,0,1:T(8,128)(2,1)S(1)} all-to-all(bf16[2,4,8,1024]{3,2,0,1:T(8,128)(2,1)S(1)} %copy.44), channel_id=1, replica_groups=mesh['heads_0'=2,'heads_1'=4,'blk'=64] {'heads_1'}, dimensions={1} | all-to-all | bytes 262144 | tf_op jit(solution)/shard_map/all_to_all | solution.py:34
  90.6 4.2 %stack.3 = bf16[64,8,8192]{2,1,0:T(8,128)(2,1)} broadcast(bf16[8,8192]{1,0:T(8,128)(2,1)S(1)} %bitcast.281), dimensions={1,2} | broadcast | bytes 8519680 | tf_op jit(solution)/shard_map/stack | solution.py:109
  94.9 24.5 %all-to-all-start.2 = ((bf16[64,8,8192]{2,1,0:T(8,128)(2,1)}), bf16[64,8,8192]{2,1,0:T(8,128)(2,1)}, u32[]{:S(2)}, u32[]{:S(2)}) async-start(bf16[64,8,8192]{2,1,0:T(8,128)(2,1)} %stack.3), calls=%async_computation.2 | async-start | bytes 16777216 | tf_op jit(solution)/shard_map/all_to_all | solution.py:109
  120.1 176.5 %all-gather.2.cloned.1.call-done = bf16[8192,256]{1,0:T(8,128)(2,1)} async-done(((bf16[1024,256]{1,0:T(8,128)(2,1)}), bf16[8192,256]{1,0:T(8,128)(2,1)}) %all-gather.2.cloned.1.call-update) | async-done | bytes 4194320 | tf_op jit(solution)/shard_map/all_gather | solution.py:80
  296.6 68.0 %all-to-all-done.2 = bf16[64,8,8192]{2,1,0:T(8,128)(2,1)} async-done(((bf16[64,8,8192]{2,1,0:T(8,128)(2,1)}), bf16[64,8,8192]{2,1,0:T(8,128)(2,1)}, u32[]{:S(2)}, u32[]{:S(2)}) %all-to-all-start.2) | async-done | bytes 8388640 | tf_op jit(solution)/shard_map/all_to_all | solution.py:109
  364.5 6.9 %fusion.38 = bf16[512,256]{1,0:T(8,128)(2,1)S(1)} fusion(bf16[8192,256]{1,0:T(8,128)(2,1)} %all-gather.2.cloned.1.call-done, bf16[64,8,8192]{2,1,0:T(8,128)(2,1)} %all-to-all-done.2), kind=kOutput, calls=%fused_computation.42 | convolution fusion | flops 2147614720 | bytes 12845056 | tf_op jit(solution)/shard_map/dot_general | solution.py:107
  371.4 29.0 %all_to_all.32 = bf16[8,8,1,8,256]{4,3,1,2,0:T(8,128)(2,1)S(1)} all-to-all(bf16[8,8,1,8,256]{4,3,1,2,0:T(8,128)(2,1)S(1)} %bitcast.282), channel_id=1, replica_groups=mesh['heads_0'=2,'heads_1'=4,'blk'=64] {'heads_0','heads_1'}, dimensions={0} | all-to-all | bytes 524288 | tf_op jit(solution)/shard_map/all_to_all | solution.py:116
  (41 shorter events, 18.7 us)
Async XLA Ops:
  6.5 17.1 %copy-start = (bf16[1,2048,128]{2,1,0:T(8,128)(2,1)S(1)}, bf16[1,2048,128]{2,1,0:T(8,128)(2,1)}, u32[]{:S(2)}) copy-start(bf16[1,2048,128]{2,1,0:T(8,128)(2,1)} %param.7) | copy-start | bytes 1572868
  7.5 18.0 %collective-permute-start.3 = (bf16[64,1,8,128]{3,0,2,1:T(8,128)(2,1)S(1)}, bf16[64,1,8,128]{3,0,2,1:T(8,128)(2,1)S(1)}, u32[]{:S(2)}, u32[]{:S(2)}) collective-permute-start(bf16[64,1,8,128]{3,0,2,1:T(8,128)(2,1)S(1)} %bitcast.283), channel_id=1, source_target_pairs={{0,2},{1,3},{2,4},{3,5},{4,6},{5,7},{6,8},{7,9},{8,10},{9,11},{10,... | collective-permute-start | bytes 393224 | tf_op jit(solution)/shard_map/ppermute | solution.py:15
  10.9 24.2 %collective-permute-start.6 = (bf16[64,1,8,128]{3,0,2,1:T(8,128)(2,1)S(1)}, bf16[64,1,8,128]{3,0,2,1:T(8,128)(2,1)S(1)}, u32[]{:S(2)}, u32[]{:S(2)}) collective-permute-start(bf16[64,1,8,128]{3,0,2,1:T(8,128)(2,1)S(1)} %bitcast.284), channel_id=1, source_target_pairs={{0,3},{1,4},{2,5},{3,6},{4,7},{5,8},{6,9},{7,10},{8,11},{9,12},{10... | collective-permute-start | bytes 393224 | tf_op jit(solution)/shard_map/ppermute | solution.py:15
  13.5 15.0 %collective-permute-start = (bf16[64,1,8,128]{3,0,2,1:T(8,128)(2,1)S(1)}, bf16[64,1,8,128]{3,0,2,1:T(8,128)(2,1)S(1)}, u32[]{:S(2)}, u32[]{:S(2)}) collective-permute-start(bf16[64,1,8,128]{3,0,2,1:T(8,128)(2,1)S(1)} %bitcast.285), channel_id=1, source_target_pairs={{0,1},{1,2},{2,3},{3,4},{4,5},{5,6},{6,7},{7,8},{8,9},{9,10},{10,1... | collective-permute-start | bytes 393224 | tf_op jit(solution)/shard_map/ppermute | solution.py:15
  25.5 1.0 copy-start.1
  31.4 15.5 %collective-permute-start.10 = (f32[64,1,8]{0,2,1:T(8,128)S(1)}, f32[64,1,8]{0,2,1:T(8,128)S(1)}, u32[]{:S(2)}, u32[]{:S(2)}) collective-permute-start(f32[64,1,8]{0,2,1:T(8,128)S(1)} %bitcast.290), channel_id=1, source_target_pairs={{0,62},{1,63},{2,0},{3,1},{4,2},{5,3},{6,4},{7,5},{8,6},{9,7},{10,... | collective-permute-start | bytes 6152 | tf_op jit(solution)/shard_map/ppermute | solution.py:15
  37.1 13.2 %collective-permute-start.11 = (f32[64,1,8]{0,2,1:T(8,128)S(1)}, f32[64,1,8]{0,2,1:T(8,128)S(1)}, u32[]{:S(2)}, u32[]{:S(2)}) collective-permute-start(f32[64,1,8]{0,2,1:T(8,128)S(1)} %bitcast.291), channel_id=1, source_target_pairs={{0,61},{1,62},{2,63},{3,0},{4,1},{5,2},{6,3},{7,4},{8,5},{9,6},{10... | collective-permute-start | bytes 6152 | tf_op jit(solution)/shard_map/ppermute | solution.py:15
  39.0 14.9 %collective-permute-start.9 = (f32[64,1,8]{0,2,1:T(8,128)S(1)}, f32[64,1,8]{0,2,1:T(8,128)S(1)}, u32[]{:S(2)}, u32[]{:S(2)}) collective-permute-start(f32[64,1,8]{0,2,1:T(8,128)S(1)} %bitcast.289), channel_id=1, source_target_pairs={{0,63},{1,0},{2,1},{3,2},{4,3},{5,4},{6,5},{7,6},{8,7},{9,8},{10,9... | collective-permute-start | bytes 6152 | tf_op jit(solution)/shard_map/ppermute | solution.py:15
  41.8 15.6 %collective-permute-start.1 = (f32[64,1,8]{0,2,1:T(8,128)S(1)}, f32[64,1,8]{0,2,1:T(8,128)S(1)}, u32[]{:S(2)}, u32[]{:S(2)}) collective-permute-start(f32[64,1,8]{0,2,1:T(8,128)S(1)} %bitcast.287), channel_id=1, source_target_pairs={{0,63},{1,0},{2,1},{3,2},{4,3},{5,4},{6,5},{7,6},{8,7},{9,8},{10,9... | collective-permute-start | bytes 6152 | tf_op jit(solution)/shard_map/ppermute | solution.py:15
  44.6 17.4 %collective-permute-start.4 = (f32[64,1,8]{0,2,1:T(8,128)S(1)}, f32[64,1,8]{0,2,1:T(8,128)S(1)}, u32[]{:S(2)}, u32[]{:S(2)}) collective-permute-start(f32[64,1,8]{0,2,1:T(8,128)S(1)} %bitcast.286), channel_id=1, source_target_pairs={{0,62},{1,63},{2,0},{3,1},{4,2},{5,3},{6,4},{7,5},{8,6},{9,7},{10,... | collective-permute-start | bytes 6152 | tf_op jit(solution)/shard_map/ppermute | solution.py:15
  46.9 15.1 %collective-permute-start.7 = (f32[64,1,8]{0,2,1:T(8,128)S(1)}, f32[64,1,8]{0,2,1:T(8,128)S(1)}, u32[]{:S(2)}, u32[]{:S(2)}) collective-permute-start(f32[64,1,8]{0,2,1:T(8,128)S(1)} %bitcast.288), channel_id=1, source_target_pairs={{0,61},{1,62},{2,63},{3,0},{4,1},{5,2},{6,3},{7,4},{8,5},{9,6},{10... | collective-permute-start | bytes 6152 | tf_op jit(solution)/shard_map/ppermute | solution.py:15
  50.3 11.7 %collective-permute-start.2 = (f32[64,1,8,128]{3,0,2,1:T(8,128)S(1)}, f32[64,1,8,128]{3,0,2,1:T(8,128)S(1)}, u32[]{:S(2)}, u32[]{:S(2)}) collective-permute-start(f32[64,1,8,128]{3,0,2,1:T(8,128)S(1)} %fusion.47), channel_id=1, source_target_pairs={{0,63},{1,0},{2,1},{3,2},{4,3},{5,4},{6,5},{7,6},{8,7},{9,8},{10,9... | collective-permute-start | bytes 786440 | tf_op jit(solution)/shard_map/ppermute | solution.py:15
  54.0 11.1 %collective-permute-start.5 = (f32[64,1,8,128]{3,0,2,1:T(8,128)S(1)}, f32[64,1,8,128]{3,0,2,1:T(8,128)S(1)}, u32[]{:S(2)}, u32[]{:S(2)}) collective-permute-start(f32[64,1,8,128]{3,0,2,1:T(8,128)S(1)} %fusion.44), channel_id=1, source_target_pairs={{0,62},{1,63},{2,0},{3,1},{4,2},{5,3},{6,4},{7,5},{8,6},{9,7},{10,... | collective-permute-start | bytes 786440 | tf_op jit(solution)/shard_map/ppermute | solution.py:15
  57.4 14.5 %collective-permute-start.8 = (f32[64,1,8,128]{3,0,2,1:T(8,128)S(1)}, f32[64,1,8,128]{3,0,2,1:T(8,128)S(1)}, u32[]{:S(2)}, u32[]{:S(2)}) collective-permute-start(f32[64,1,8,128]{3,0,2,1:T(8,128)S(1)} %fusion.41), channel_id=1, source_target_pairs={{0,61},{1,62},{2,63},{3,0},{4,1},{5,2},{6,3},{7,4},{8,5},{9,6},{10... | collective-permute-start | bytes 786440 | tf_op jit(solution)/shard_map/ppermute | solution.py:15
  94.9 269.7 %all-to-all-start.2 = ((bf16[64,8,8192]{2,1,0:T(8,128)(2,1)}), bf16[64,8,8192]{2,1,0:T(8,128)(2,1)}, u32[]{:S(2)}, u32[]{:S(2)}) async-start(bf16[64,8,8192]{2,1,0:T(8,128)(2,1)} %stack.3), calls=%async_computation.2 | async-start | bytes 16777216 | tf_op jit(solution)/shard_map/all_to_all | solution.py:109
  119.3 177.2 %all-gather.2.cloned.1.call-start = ((), (), s32[]{:S(2)}) async-start(), calls=%async_computation.4 | async-start | bytes 4718592 | tf_op jit(solution)/shard_map/all_gather | solution.py:80
Sparse Core Ops, SparseCore 0:
  122.2 174.3 all-gather.1
